TPU v7x, 32 devices: a whole 2x2x4 slice. The times are simulated.
32 devices in a mesh: gx: 4 (over y, core), gy: 8 (over z, x).
Axes of the slice: x: 2, y: 2, z: 4, core: 2. Of those that a mesh axis runs over, the one named last changes fastest.
Arguments:
- hidden_states: bfloat16 [1024, 128], replicated, may hold values from -60 to 60
- item_table: bfloat16 [262144, 128], P(('gx', 'gy')), may hold values from -1.796875 to 1.796875
- targets: int32 [1024], replicated, may hold values from 0 to 262143
Outputs:
- expected: float32 [1024, 128], P(('gx', 'gy'))
- nll: float32 [1024], P(('gx', 'gy'))
All inputs are finite; a program needn't handle non-finite values.
Results may differ from a plain program's by a relative error of at most 0.0023.
Values sent between devices are 32-bit elements; how exact they have to be, the bound alone decides.
A program may use at most 64 MiB of HBM per device.

v0:
```python
import functools

import jax
import jax.numpy as jnp
from jax import lax
from jax.experimental import pallas as pl
from jax.experimental.pallas import tpu as pltpu
from jax.sharding import PartitionSpec as P

AXES = ("gx", "gy")
BLOCK = 4096
SUB = 256
PARTS = 8
DEPTH = 512
MESH = pl.DeviceIdType.MESH
NT = (((1,), (1,)), ((), ()))


def kernel(ngx, ngy, rows, hid, table, tgt, packed,
           tab, tabt, held, acc, give, take, send, recv, give_sem, take_sem, send_sem, recv_sem, load_sem):
    CHUNK = rows * ngy
    positions, width = hid.shape
    items = table.shape[0]
    part = items // PARTS
    loads = []
    for i in range(PARTS):
        at = pl.ds(i * part, part)
        loads.append(pltpu.make_async_copy(table.at[at], tab.at[at], load_sem.at[i]))
        loads[i].start()
    nchunk = positions // CHUNK
    nblock = items // BLOCK
    stat_row = send.shape[1] - 8
    gx = lax.axis_index("gx")
    gy = lax.axis_index("gy")
    me = gx * ngy + gy
    core, line = lax.rem(gx, 2), gx // 2
    half = ngx // 2 * ngy
    place_of_me = line * ngy + gy
    partner = (gx + 1 - 2 * core, gy)

    barrier = pltpu.get_barrier_semaphore()

    def greet(k, c):
        other = lax.rem(place_of_me + k, half)
        pl.semaphore_signal(barrier, inc=1, device_id=(other // ngy * 2 + core, lax.rem(other, ngy)), device_id_type=MESH)
        return c

    lax.fori_loop(1, half, greet, 0)
    pl.semaphore_signal(barrier, inc=1, device_id=partner, device_id_type=MESH)

    def turn(base, count):
        at = pl.ds(base, count)
        tabt[0:width, at] = tab[at, :].T

    tabt[width:, :] = jnp.ones((tabt.shape[0] - width, items), jnp.bfloat16)

    sub_iota = lax.broadcasted_iota(jnp.int32, (8, CHUNK), 0)

    def chunk_of(k):
        mine = lax.rem(k, 2)
        return lax.rem(line + 1 + k // 2, nchunk // 2) * 2 + mine * core + (1 - mine) * (1 - core)

    def score(chunk, block, sub):
        at = pl.multiple_of(chunk * CHUNK, CHUNK)
        base = pl.multiple_of(block * BLOCK + sub * SUB, SUB)
        s = lax.dot_general(tab[pl.ds(base, SUB), :], hid[pl.ds(at, CHUNK), :], NT, preferred_element_type=jnp.float32)
        held[sub * SUB:(sub + 1) * SUB, :] = s
        return functools.reduce(jnp.maximum, [s[8 * g:8 * g + 8] for g in range(SUB // 8)])

    def top_of(tops):
        return jnp.max(functools.reduce(jnp.maximum, tops), axis=0, keepdims=True)

    def step(k, place, turning, j, carry):
        top, highest, hit = carry
        new = jnp.maximum(highest, top)
        retain = jnp.exp(highest - new)
        here = place - j * BLOCK
        later = k * nblock + j + 1
        chunk, block = chunk_of(later // nblock), lax.rem(later, nblock)
        tops, added = [], None
        for q in range(BLOCK // DEPTH):
            base = pl.multiple_of(j * BLOCK + q * DEPTH, DEPTH)
            if turning:
                turn(base, DEPTH)
            s = held[q * DEPTH:(q + 1) * DEPTH, :]
            for g in range(DEPTH // 8):
                hit = jnp.where(here == q * DEPTH + 8 * g, s[8 * g:8 * g + 8], hit)
            p = jnp.exp(s - new).astype(jnp.bfloat16)
            part = jnp.dot(tabt[:, pl.ds(base, DEPTH)], p, preferred_element_type=jnp.float32)
            added = part if added is None else added + part
            for sub in range(q * DEPTH // SUB, (q + 1) * DEPTH // SUB):
                tops.append(score(chunk, block, sub))
        acc[...] = acc[...] * retain + added
        return top_of(tops), new, hit

    def one_chunk(turning, k, top):
        chunk = chunk_of(k)
        at = pl.multiple_of(chunk * CHUNK, CHUNK)
        place = tgt[0:1, pl.ds(at, CHUNK)] - me * items - sub_iota
        acc[...] = jnp.zeros_like(acc)
        top, highest, hit = lax.fori_loop(
            0, nblock, functools.partial(step, k, place, turning),
            (top, jnp.full((1, CHUNK), -1e30, jnp.float32), jnp.zeros((8, CHUNK), jnp.float32)))
        return top, highest, jnp.sum(hit, axis=0, keepdims=True)

    def passing(k):
        return pltpu.make_async_remote_copy(
            src_ref=give.at[k // 2], dst_ref=take.at[k // 2], send_sem=give_sem.at[k // 2], recv_sem=take_sem.at[k // 2],
            device_id=partner, device_id_type=MESH)

    def two_chunks(turning, kk, top):
        top, highest, hit = one_chunk(turning, 2 * kk, top)
        give[kk, 0:width + 8, :] = acc[0:width + 8, :]
        give[kk, width + 8:, :] = jnp.concatenate([highest, hit, jnp.zeros((6, CHUNK), jnp.float32)], axis=0)
        passing(2 * kk).start()
        top, highest, hit = one_chunk(False, 2 * kk + 1, top)
        passing(2 * kk).wait_recv()
        other = take[kk, width + 8:width + 9, :]
        both = jnp.maximum(highest, other)
        own_share, other_share = jnp.exp(highest - both), jnp.exp(other - both)
        weighted = (acc[0:width, :] * own_share + take[kk, 0:width, :] * other_share).T
        total = acc[width:width + 1, :] * own_share + take[kk, width:width + 1, :] * other_share
        stats = jnp.concatenate(
            [both, total, hit + take[kk, width + 9:width + 10, :], jnp.zeros((5, CHUNK), jnp.float32)], axis=0)
        chunk = chunk_of(2 * kk + 1)
        for o in range(ngy):
            owner = chunk // 2 * ngy + o
            send[owner, 0:rows, :] = weighted[o * rows:(o + 1) * rows, :]
            turned = stats if o == 0 else pltpu.roll(stats, CHUNK - o * rows, 1)
            send[owner, stat_row:, :] = turned[:, 0:width]
        for o in range(ngy):
            owner = chunk // 2 * ngy + o

            @pl.when(owner != place_of_me)
            def _():
                slot = lax.rem(place_of_me - owner - 1 + half, half)
                pltpu.make_async_remote_copy(
                    src_ref=send.at[owner], dst_ref=recv.at[slot], send_sem=send_sem, recv_sem=recv_sem,
                    device_id=(chunk, o), device_id_type=MESH).start()
        return top

    tops = []
    for i in range(PARTS):
        loads[i].wait()
        tops += [score(chunk_of(0), 0, sub) for sub in range(BLOCK // SUB) if sub * SUB // part == i]
    top = top_of(tops)
    pl.semaphore_wait(barrier, half)
    top = two_chunks(True, 0, top)
    lax.fori_loop(1, nchunk // 2, functools.partial(two_chunks, False), top)

    def given(kk, c):
        passing(2 * kk).wait_send()
        return c

    lax.fori_loop(0, nchunk // 2, given, 0)
    recv[half - 1] = send[place_of_me]
    most = recv.at[pl.ds(0, half - 1)]
    whole = pltpu.make_async_remote_copy(
        src_ref=most, dst_ref=most, send_sem=send_sem, recv_sem=recv_sem,
        device_id=(gx, gy), device_id_type=MESH)
    whole.wait_send()
    whole.wait_recv()

    tops = recv[:, stat_row, :]
    top = jnp.max(tops, axis=0, keepdims=True)
    factor = jnp.exp(tops - top)
    total = jnp.sum(factor * recv[:, stat_row + 1, :], axis=0, keepdims=True)
    target = jnp.sum(recv[:, stat_row + 2, :], axis=0, keepdims=True)
    packed[stat_row:stat_row + 1, :] = top + jnp.log(total) - target
    share = (factor / total).T
    out = jnp.zeros((rows, width), jnp.float32)
    for s in range(half):
        out = out + share[0:rows, s:s + 1] * recv[s, 0:rows, :]
    packed[0:rows, :] = out


def unpack(rows, stat_row, packed, exp_out, nll_out):
    exp_out[...] = packed[0:rows, :]
    nll_out[...] = packed[stat_row, 0:rows]


def solution(mesh):
    n = mesh.size
    ngx, ngy = mesh.shape["gx"], mesh.shape["gy"]

    def local(hidden_states, item_table, targets):
        positions, width = hidden_states.shape
        items = item_table.shape[0]
        rows = positions // n
        chunk = rows * ngy
        tall = -(-rows // 8) * 8 + 8
        vmem = pl.BlockSpec(memory_space=pltpu.VMEM)
        packed = pl.pallas_call(
            functools.partial(kernel, ngx, ngy, rows),
            out_shape=jax.ShapeDtypeStruct((tall, width), jnp.float32),
            in_specs=[vmem, pl.BlockSpec(memory_space=pl.ANY), vmem],
            out_specs=vmem,
            scratch_shapes=[
                pltpu.VMEM((items, width), jnp.bfloat16),
                pltpu.VMEM((width + 16, items), jnp.bfloat16),
                pltpu.VMEM((BLOCK, chunk), jnp.float32),
                pltpu.VMEM((width + 16, chunk), jnp.float32),
                pltpu.VMEM((ngx // 2, width + 16, chunk), jnp.float32),
                pltpu.VMEM((ngx // 2, width + 16, chunk), jnp.float32),
                pltpu.VMEM((n // 2, tall, width), jnp.float32),
                pltpu.VMEM((n // 2, tall, width), jnp.float32),
                pltpu.SemaphoreType.DMA((ngx // 2,)),
                pltpu.SemaphoreType.DMA((ngx // 2,)),
                pltpu.SemaphoreType.DMA,
                pltpu.SemaphoreType.DMA,
                pltpu.SemaphoreType.DMA((PARTS,)),
            ],
            compiler_params=pltpu.CompilerParams(collective_id=0, has_side_effects=True, vmem_limit_bytes=60000000),
        )(hidden_states, item_table, targets.reshape(1, positions))
        return pl.pallas_call(
            functools.partial(unpack, rows, tall - 8),
            out_shape=(jax.ShapeDtypeStruct((rows, width), jnp.float32), jax.ShapeDtypeStruct((rows,), jnp.float32)),
            in_specs=[vmem], out_specs=(vmem, vmem),
        )(packed)

    return jax.shard_map(
        local, mesh=mesh,
        in_specs=(P(), P(AXES, None), P()),
        out_specs=(P(AXES, None), P(AXES)),
        check_vma=False,
    )
```

profile of v0, /device:TPU:0, one launch (start us, length us, event | category | flops | bytes accessed | tf_op | source)
XLA Modules:
  0.0 24.7 jit_solution(18091494230493487487)
XLA Ops:
  0.6 22.7 %shard_map.50.packed = f32[40,128]{1,0:T(8,128)} custom-call(bf16[1024,128]{1,0:T(8,128)(2,1)} %hid.1, bf16[8192,128]{1,0:T(8,128)(2,1)} %table.1, s32[1,1024]{1,0:T(1,128)} %bitcast.1), custom_call_target="tpu_custom_call" | custom-call | tf_op jit(solution)/shard_map/pallas_call | solution.py:193
  23.4 1.3 %shard_map.51 = (f32[32,128]{1,0:T(8,128)}, f32[32]{0:T(128)}) custom-call(f32[40,128]{1,0:T(8,128)} %shard_map.50.packed), custom_call_target="tpu_custom_call" | custom-call | tf_op jit(solution)/shard_map/pallas_call | solution.py:215
where the time goes:
time: 24.9 us; the launch traced here: 24.7 us
  Pallas kernels  24.1 us (97%)
  between operations  0.64 us (3%)
    pallas_call x1, Pallas kernels, local(): pl.pallas_call(functools.partial(kernel, ngx, ngy, rows), out_shape=jax.S...  22.7 us
    pallas_call x1, Pallas kernels, local(): pl.pallas_call(functools.partial(unpack, rows, tall - 8), out_shape=(jax....  1.34 us

commit v1 on v0

v1 whole, which is shorter than its diff:
```python
import functools

import jax
import jax.numpy as jnp
from jax import lax
from jax.experimental import pallas as pl
from jax.experimental.pallas import tpu as pltpu
from jax.sharding import PartitionSpec as P

AXES = ("gx", "gy")
BLOCK = 2048
SUB = 256
DEPTH = 512
LEAD = 4
PARTS = 8
CORES = 2
MESH = pl.DeviceIdType.MESH
NT = (((1,), (1,)), ((), ()))


def kernel(ngx, ngy, rows, hid, table, targets, packed,
           hall, hk, tgt, spots, tgt_now, tab, wide, tabt, even, odd, stage, acc, give, take, send, recv,
           give_sem, take_sem, send_sem, recv_sem, load_sem, small_sem):
    positions, width = hid.shape
    items = table.shape[0]
    part = items // PARTS
    lines, side = ngx // CORES, ngy // 2
    half = lines * ngy
    owners = lines * side
    seg = side * rows
    chunk = lines * seg
    stat_row = send.shape[2] - 8
    gx = lax.axis_index("gx")
    gy = lax.axis_index("gy")
    me = gx * ngy + gy
    core, line = lax.rem(gx, CORES), gx // CORES
    zone, spot = gy // side, lax.rem(gy, side)
    place_of_me = line * ngy + gy
    partner = (gx + 1 - 2 * core, gy)

    hid_load = pltpu.make_async_copy(hid, hall, small_sem.at[0])
    hid_load.start()
    loads = []
    for i in range(PARTS):
        at = pl.ds(i * part, part)
        loads.append(pltpu.make_async_copy(table.at[at], tab.at[at], load_sem.at[i]))
        loads[i].start()
    tgt_load = pltpu.make_async_copy(targets, tgt, small_sem.at[1])
    tgt_load.start()

    even[0:8, :] = jnp.zeros((8, chunk), jnp.float32)
    odd[0:8, :] = jnp.zeros((8, chunk), jnp.float32)
    barrier = pltpu.get_barrier_semaphore()

    def greet(k, c):
        other = lax.rem(place_of_me + k, half)
        pl.semaphore_signal(barrier, inc=1, device_id=(other // ngy * CORES + core, lax.rem(other, ngy)),
                            device_id_type=MESH)
        return c

    lax.fori_loop(1, half, greet, 0)
    pl.semaphore_signal(barrier, inc=1, device_id=partner, device_id_type=MESH)

    tabt[width:, :] = jnp.ones((tabt.shape[0] - width, items), jnp.bfloat16)
    wide[items:, :] = jnp.zeros((8, width), jnp.float32)

    def owner_core(k):
        return core if k % 2 else 1 - core

    def owner_zone(k):
        return zone if k >= 2 else 1 - zone

    def start_of(k, y):
        return ((y * CORES + owner_core(k)) * ngy + owner_zone(k) * side) * rows

    def held_of(base):
        b = base // BLOCK
        return (odd if b % 2 else even), base - b * BLOCK

    def score(k, base):
        x = tab[base:base + SUB, :]
        if k == 0:
            wide[base:base + SUB, :] = x.astype(jnp.float32)
        s = lax.dot_general(x, hk[k], NT, preferred_element_type=jnp.float32)
        held, at = held_of(base)
        held[at:at + SUB, :] = s
        return functools.reduce(jnp.maximum, [s[8 * g:8 * g + 8] for g in range(SUB // 8)])

    def top_of(tops):
        return jnp.max(functools.reduce(jnp.maximum, tops), axis=0, keepdims=True)

    def turn(base):
        tabt[0:width, base:base + DEPTH] = tab[base:base + DEPTH, :].T

    def weigh(k, base, new):
        if k == 0:
            turn(base)
        held, at = held_of(base)
        p = jnp.exp(held[at:at + DEPTH, :] - new).astype(jnp.bfloat16)
        return jnp.dot(tabt[:, base:base + DEPTH], p, preferred_element_type=jnp.float32)

    def fetch(k, lo, hi):
        for i in range(lo, hi):
            y, r = i // seg, i % seg
            t = tgt_now[k * lines + y, r]
            stage[i:i + 1, :] = wide[pl.ds(t, 1), :]

    def hits(k):
        return jnp.sum((stage[...] * hk[k].astype(jnp.float32)).T, axis=0, keepdims=True)

    def passing(kk):
        return pltpu.make_async_remote_copy(
            src_ref=give.at[kk], dst_ref=take.at[kk], send_sem=give_sem.at[kk], recv_sem=take_sem.at[kk],
            device_id=partner, device_id_type=MESH)

    def hand_over(kk, highest, hit):
        if kk == 0:
            pl.semaphore_wait(barrier, half)
        give[kk, 0:width, :] = acc[0:width, :]
        give[kk, width:, :] = jnp.concatenate(
            [acc[width:width + 1, :], highest, hit, jnp.zeros((5, chunk), jnp.float32)], axis=0)
        passing(kk).start()

    def send_out(kk, highest, hit):
        passing(kk).wait_recv()
        other = take[kk, width + 1:width + 2, :]
        both = jnp.maximum(highest, other)
        own_share, other_share = jnp.exp(highest - both), jnp.exp(other - both)
        weighted = (acc[0:width, :] * own_share + take[kk, 0:width, :] * other_share).T
        total = acc[width:width + 1, :] * own_share + take[kk, width:width + 1, :] * other_share
        stats = jnp.concatenate(
            [both, total, hit + take[kk, width + 2:width + 3, :], jnp.zeros((5, chunk), jnp.float32)], axis=0)
        for o in range(owners):
            send[kk, o, 0:rows, :] = weighted[o * rows:(o + 1) * rows, :]
            turned = stats if o == 0 else pltpu.roll(stats, chunk - o * rows, 1)
            send[kk, o, stat_row:, :] = turned[:, 0:width]
        for o in range(owners):
            to_line, to_gy = o // side, owner_zone(2 * kk) * side + o % side
            slot = lax.rem(place_of_me - (to_line * ngy + to_gy) - 1 + half, half)
            copy = pltpu.make_async_remote_copy(
                src_ref=send.at[kk, o], dst_ref=recv.at[slot], send_sem=send_sem, recv_sem=recv_sem,
                device_id=(to_line * CORES + core, to_gy), device_id_type=MESH)
            if kk == 0:
                copy.start()
            else:
                pl.when(o != line * side + spot)(copy.start)

    blocks = [(k, b * BLOCK) for k in range(4) for b in range(items // BLOCK)]
    tgt_load.wait()
    for k in range(4):
        for y in range(lines):
            t = tgt[pl.ds(start_of(k, y) // seg, 1), :] - me * items
            spots[k * lines + y:k * lines + y + 1, :] = jnp.where(jnp.logical_and(t >= 0, t < items), t, items)
    hid_load.wait()
    for k in range(4):
        for y in range(lines):
            hk[k, y * seg:(y + 1) * seg, :] = hall[pl.ds(pl.multiple_of(start_of(k, y), seg), seg), :]

    def subs_of(n):
        if n >= len(blocks):
            return []
        k, base = blocks[n]
        return [(k, base + i * SUB) for i in range(BLOCK // SUB)]

    tops = []
    waited = 0
    for k, base in subs_of(0):
        while waited * part < base + SUB:
            loads[waited].wait()
            waited += 1
        tops.append(score(k, base))

    spot_copy = pltpu.make_async_copy(spots, tgt_now, small_sem.at[1])
    spot_copy.start()
    for n, (k, base) in enumerate(blocks):
        top = top_of(tops)
        if n == 1:
            spot_copy.wait()
        first, last = base == 0, base + BLOCK == items
        new = top if first else jnp.maximum(highest, top)
        ahead = subs_of(n + 1)
        tops = []
        if ahead:
            while waited < PARTS and waited * part < ahead[-1][1] + SUB:
                loads[waited].wait()
                waited += 1
        count = BLOCK // DEPTH
        added = None
        for q in range(count + 1):
            upto = len(ahead) if q == count else min(len(ahead), LEAD + len(ahead) * q // count)
            while len(tops) < upto:
                tops.append(score(*ahead[len(tops)]))
            if q < count:
                piece = weigh(k, base + q * DEPTH, new)
                added = piece if added is None else added + piece
                at = base // BLOCK * count + q
                steps = items // DEPTH
                if k == 0:
                    at, steps = at - steps + count, count
                if at >= 0:
                    fetch(k, at * chunk // steps, (at + 1) * chunk // steps)
        acc[...] = added if first else acc[...] * jnp.exp(highest - new) + added
        highest = new
        if last:
            (send_out if k % 2 else hand_over)(k // 2, highest, hits(k))

    for kk in range(2):
        passing(kk).wait_send()
    recv[half - 1] = send[1, line * side + spot]
    most = recv.at[pl.ds(0, half - 1)]
    whole = pltpu.make_async_remote_copy(
        src_ref=most, dst_ref=most, send_sem=send_sem, recv_sem=recv_sem,
        device_id=(gx, gy), device_id_type=MESH)
    whole.wait_send()
    whole.wait_recv()

    tops = recv[:, stat_row, :]
    top = jnp.max(tops, axis=0, keepdims=True)
    factor = jnp.exp(tops - top)
    total = jnp.sum(factor * recv[:, stat_row + 1, :], axis=0, keepdims=True)
    target = jnp.sum(recv[:, stat_row + 2, :], axis=0, keepdims=True)
    packed[stat_row:stat_row + 1, :] = top + jnp.log(total) - target
    share = (factor / total).T
    out = jnp.zeros((rows, width), jnp.float32)
    for s in range(half):
        out = out + share[0:rows, s:s + 1] * recv[s, 0:rows, :]
    packed[0:rows, :] = out


def unpack(rows, stat_row, packed, exp_out, nll_out):
    exp_out[...] = packed[0:rows, :]
    nll_out[...] = packed[stat_row, 0:rows]


def solution(mesh):
    n = mesh.size
    ngx, ngy = mesh.shape["gx"], mesh.shape["gy"]

    def local(hidden_states, item_table, targets):
        positions, width = hidden_states.shape
        items = item_table.shape[0]
        rows = positions // n
        half = n // CORES
        chunk = positions // 4
        seg = chunk // (ngx // CORES)
        tall = -(-rows // 8) * 8 + 8
        vmem = pl.BlockSpec(memory_space=pltpu.VMEM)
        far = pl.BlockSpec(memory_space=pl.ANY)
        packed = pl.pallas_call(
            functools.partial(kernel, ngx, ngy, rows),
            out_shape=pltpu.VMEM((tall, width), jnp.float32),
            in_specs=[far, far, far],
            out_specs=vmem,
            scratch_shapes=[
                pltpu.VMEM((positions, width), jnp.bfloat16),
                pltpu.VMEM((4, chunk, width), jnp.bfloat16),
                pltpu.VMEM((positions // seg, seg), jnp.int32),
                pltpu.VMEM((positions // seg, seg), jnp.int32),
                pltpu.SMEM((positions // seg, seg), jnp.int32),
                pltpu.VMEM((items, width), jnp.bfloat16),
                pltpu.VMEM((items + 8, width), jnp.float32),
                pltpu.VMEM((width + 16, items), jnp.bfloat16),
                pltpu.VMEM((BLOCK, chunk), jnp.float32),
                pltpu.VMEM((BLOCK, chunk), jnp.float32),
                pltpu.VMEM((chunk, width), jnp.float32),
                pltpu.VMEM((width + 16, chunk), jnp.float32),
                pltpu.VMEM((2, width + 8, chunk), jnp.float32),
                pltpu.VMEM((2, width + 8, chunk), jnp.float32),
                pltpu.VMEM((2, half // 2, tall, width), jnp.float32),
                pltpu.VMEM((half, tall, width), jnp.float32),
                pltpu.SemaphoreType.DMA((2,)),
                pltpu.SemaphoreType.DMA((2,)),
                pltpu.SemaphoreType.DMA,
                pltpu.SemaphoreType.DMA,
                pltpu.SemaphoreType.DMA((PARTS,)),
                pltpu.SemaphoreType.DMA((2,)),
            ],
            compiler_params=pltpu.CompilerParams(collective_id=0, has_side_effects=True, vmem_limit_bytes=60000000),
        )(hidden_states, item_table, targets.reshape(positions // seg, seg))
        packed = pltpu.with_memory_space_constraint(packed, pltpu.VMEM)
        return pl.pallas_call(
            functools.partial(unpack, rows, tall - 8),
            out_shape=(jax.ShapeDtypeStruct((rows, width), jnp.float32), jax.ShapeDtypeStruct((rows,), jnp.float32)),
            in_specs=[vmem], out_specs=(vmem, vmem),
        )(packed)

    return jax.shard_map(
        local, mesh=mesh,
        in_specs=(P(), P(AXES, None), P()),
        out_specs=(P(AXES, None), P(AXES)),
        check_vma=False,
    )
```

time: 24.9 us -> 20.7 us (0.83)
  Pallas kernels: 24.1 us -> 19.9 us
    pallas_call x1, Pallas kernels: 22.7 us -> 19.3 us  [local(): pl.pallas_call(functools.partial(kernel, ngx, ngy, rows), out_shape=pltpu...]
    pallas_call x1, Pallas kernels: 1.34 us -> 0.61 us  [local(): pl.pallas_call(functools.partial(unpack, rows, tall - 8), out_shape=(jax....]
where the time goes in v1:
time: 20.7 us; the launch traced here: 20.5 us
  Pallas kernels  19.9 us (96%)
  between operations  0.64 us (3%)
    pallas_call x1, Pallas kernels, local(): pl.pallas_call(functools.partial(kernel, ngx, ngy, rows), out_shape=pltpu...  19.3 us
    pallas_call x1, Pallas kernels, local(): pl.pallas_call(functools.partial(unpack, rows, tall - 8), out_shape=(jax....  0.61 us

profile of v1, /device:TPU:0, one launch (start us, length us, event | category | flops | bytes accessed | tf_op | source)
XLA Modules:
  0.0 20.5 jit_solution(834552024201047917)
XLA Ops:
  0.6 19.3 %shard_map.50.packed = f32[40,128]{1,0:T(8,128)S(1)} custom-call(bf16[1024,128]{1,0:T(8,128)(2,1)} %hid.1, bf16[8192,128]{1,0:T(8,128)(2,1)} %table.1, s32[8,128]{1,0:T(8,128)} %bitcast.1), custom_call_target="tpu_custom_call" | custom-call | tf_op jit(solution)/shard_map/pallas_call | solution.py:249
  19.9 0.6 %shard_map.51 = (f32[32,128]{1,0:T(8,128)}, f32[32]{0:T(128)}) custom-call(f32[40,128]{1,0:T(8,128)S(1)} %shard_map.50.packed), custom_call_target="tpu_custom_call" | custom-call | tf_op jit(solution)/shard_map/pallas_call | solution.py:281

commit v2 on v1

v2 whole, which is shorter than its diff:
```python
import functools

import jax
import jax.numpy as jnp
from jax import lax
from jax.experimental import pallas as pl
from jax.experimental.pallas import tpu as pltpu
from jax.sharding import PartitionSpec as P

AXES = ("gx", "gy")
BLOCK = 2048
SUB = 256
DEPTH = 512
LEAD = 3
HOLD = 1
LOG2E = 1.4426950408889634
PARTS = 8
ZONES = 4
MESH = pl.DeviceIdType.MESH
NT = (((1,), (1,)), ((), ()))


def kernel(ngx, ngy, rows, hid, table, targets, packed,
           hall, hk, both, tgt, spots, tgt_now, tab, wide, tabt, even, odd, stage, acc, send, recv, mid, last,
           send_sem, recv_sem, mid_sem, last_sem, load_sem, small_sem):
    positions, width = hid.shape
    items = table.shape[0]
    part = items // PARTS
    side = ngy // ZONES
    members = ngx * side
    seg = side * rows
    chunk = ngx * seg
    stat_row = send.shape[2] - 8
    used = pl.ds(0, stat_row + 3)
    gx = lax.axis_index("gx")
    gy = lax.axis_index("gy")
    me = gx * ngy + gy
    zone, spot = gy // side, lax.rem(gy, side)
    upper = zone // 2
    zones = (3 - 3 * upper, 2 - upper, zone + 1 - 2 * lax.rem(zone, 2), zone)
    shifts = sorted(((a, b) for a in range(ngx) for b in range(side) if a or b), key=lambda ab: (-(ab[0] > 0) - (ab[1] > 0), ab))

    def peer(a, b):
        return (lax.rem(gx + a, ngx), zone * side + lax.rem(spot + b, side))

    def slot_of(a, b):
        return a * side + b - 1

    def twin(k):
        return (gx, zones[k] * side + spot)

    tgt_load = pltpu.make_async_copy(targets, tgt, small_sem.at[1])
    tgt_load.start()
    hid_load = pltpu.make_async_copy(hid, hall, small_sem.at[0])
    hid_load.start()
    loads = []
    for i in range(PARTS):
        at = pl.ds(i * part, part)
        loads.append(pltpu.make_async_copy(table.at[at], tab.at[at], load_sem.at[i]))
        loads[i].start()

    even[0:8, :] = jnp.zeros((8, chunk), jnp.float32)
    odd[0:8, :] = jnp.zeros((8, chunk), jnp.float32)
    barrier = pltpu.get_barrier_semaphore()

    def greet(j, c):
        pl.semaphore_signal(barrier, inc=1, device_id=peer(j // side, lax.rem(j, side)), device_id_type=MESH)
        return c

    lax.fori_loop(1, members, greet, 0)
    for k in range(ZONES - 1):
        pl.semaphore_signal(barrier, inc=1, device_id=twin(k), device_id_type=MESH)

    tabt[width:, :] = jnp.ones((tabt.shape[0] - width, items), jnp.bfloat16)
    wide[items:, :] = jnp.zeros((8, width), jnp.float32)

    def start_of(k, g):
        return (g * ngy + zones[k] * side) * rows

    blocks = []
    for k in range(ZONES):
        sizes = [BLOCK] * (items // BLOCK)
        if k == 0:
            sizes[:1] = [BLOCK // 2]
            sizes.append(BLOCK // 2)
        elif k == ZONES - 1:
            sizes[-1:] = [BLOCK // 2] * 2
        blocks += [(k, sum(sizes[:i]), size) for i, size in enumerate(sizes)]

    def held_of(n):
        return odd if n % 2 else even

    def widen(lo, hi):
        wide[lo:hi, :] = tab[lo:hi, :].astype(jnp.float32)

    early = (blocks[0][2] + blocks[1][2]) // DEPTH
    edges = [blocks[0][2] + (items - blocks[0][2]) // 16 * i // early * 16 for i in range(early + 1)]

    def score(n, at):
        k, base = blocks[n][0], blocks[n][1] + at
        x = tab[base:base + SUB, :]
        if n == 0:
            widen(base, base + SUB)
        s = jnp.dot(jnp.concatenate([x, x], axis=1), both[k], preferred_element_type=jnp.float32)
        held_of(n)[at:at + SUB, :] = s
        return functools.reduce(jnp.maximum, [s[8 * g:8 * g + 8] for g in range(SUB // 8)])

    def top_of(tops):
        return jnp.max(functools.reduce(jnp.maximum, tops), axis=0, keepdims=True)

    def turn(base):
        tabt[0:width, base:base + DEPTH] = tab[base:base + DEPTH, :].T

    def weigh(n, at, new):
        k, base = blocks[n][0], blocks[n][1] + at
        if k == 0:
            turn(base)
        p = jnp.exp2(held_of(n)[at:at + DEPTH, :] - new).astype(jnp.bfloat16)
        return jnp.dot(tabt[:, base:base + DEPTH], p, preferred_element_type=jnp.float32)

    def fetch(k, lo, hi):
        for i in range(lo, hi):
            stage[k % 2, i:i + 1, :] = wide[pl.ds(tgt_now[k * ngx + i // seg, i % seg], 1), :]

    def hits(k):
        return jnp.sum((stage[k % 2] * hk[k].astype(jnp.float32)).T, axis=0, keepdims=True)

    def sending(k, a, b):
        to = lax.rem(gx + a, ngx) * side + lax.rem(spot + b, side)
        return pltpu.make_async_remote_copy(
            src_ref=send.at[k, to, used], dst_ref=(recv.at[k] if k < ZONES - 1 else last).at[slot_of(a, b), used],
            send_sem=send_sem, recv_sem=recv_sem.at[k], device_id=peer(a, b), device_id_type=MESH)

    def crossing(k):
        slot = members - 1 + lax.rem(zone - zones[k] - 1 + ZONES, ZONES)
        return pltpu.make_async_remote_copy(
            src_ref=mid.at[k, used], dst_ref=last.at[slot, used], send_sem=mid_sem, recv_sem=last_sem,
            device_id=twin(k), device_id_type=MESH)

    def send_out(k, highest, hit):
        weighted = acc[0:width, :].T
        stats = jnp.concatenate([highest, acc[width:width + 1, :], hit, jnp.zeros((5, chunk), jnp.float32)], axis=0)
        for m in range(members):
            send[k, m, 0:rows, :] = weighted[m * rows:(m + 1) * rows, :]
            turned = stats if m == 0 else pltpu.roll(stats, chunk - m * rows, 1)
            send[k, m, stat_row:, :] = turned[:, 0:width]
        if k == 0:
            pl.semaphore_wait(barrier, members - 1 + ZONES - 1)
        for a, b in shifts:
            sending(k, a, b).start()

    def merge(parts):
        tops = parts[:, stat_row, :]
        top = jnp.max(tops, axis=0, keepdims=True)
        factor = jnp.exp2(tops - top)
        total = jnp.sum(factor * parts[:, stat_row + 1, :], axis=0, keepdims=True)
        target = jnp.sum(parts[:, stat_row + 2, :], axis=0, keepdims=True)
        return top, total, target, factor

    def gather(parts, share):
        share = share.T
        out = share[0:rows, 0:1] * parts[0, 0:rows, :]
        for s in range(1, parts.shape[0]):
            out = out + share[0:rows, s:s + 1] * parts[s, 0:rows, :]
        return out

    def arrived(k):
        most = (recv.at[k] if k < ZONES - 1 else last).at[pl.ds(0, members - 1), used]
        return pltpu.make_async_remote_copy(
            src_ref=most, dst_ref=most, send_sem=send_sem, recv_sem=recv_sem.at[k],
            device_id=(gx, gy), device_id_type=MESH)

    def relay(k):
        recv[k, members - 1] = send[k, gx * side + spot]
        arrived(k).wait_recv()
        parts = recv.at[k]
        top, total, target, factor = merge(parts)
        mid[k, 0:rows, :] = gather(parts, factor)
        mid[k, stat_row:, :] = jnp.concatenate([top, total, target, jnp.zeros((5, width), jnp.float32)], axis=0)
        crossing(k).start()

    tgt_load.wait()
    for k in range(ZONES):
        for g in range(ngx):
            at = start_of(k, g)
            t = tgt[pl.ds(at // width, 1), :] - me * items
            t = jnp.where(jnp.logical_and(t >= 0, t < items), t, items)
            spots[k * ngx + g:k * ngx + g + 1, :] = pltpu.roll(t, lax.rem(width - lax.rem(at, width), width), 1)
    hid_load.wait()
    def prepare(k):
        parts = []
        for g in range(ngx):
            h = hall[pl.ds(pl.multiple_of(start_of(k, g), seg), seg), :]
            hk[k, g * seg:(g + 1) * seg, :] = h
            scaled = h.astype(jnp.float32) * LOG2E
            high = scaled.astype(jnp.bfloat16)
            parts.append(jnp.concatenate([high, (scaled - high.astype(jnp.float32)).astype(jnp.bfloat16)], axis=1))
        both[k] = jnp.concatenate(parts, axis=0).T

    prepare(0)
    spot_copy = pltpu.make_async_copy(spots, tgt_now, small_sem.at[1])
    spot_copy.start()

    def subs_of(n):
        return [(n, i * SUB) for i in range(blocks[n][2] // SUB)] if n < len(blocks) else []

    tops = []
    drawn = None
    waited = 0
    for n, at in subs_of(0):
        while waited * part < at + SUB:
            loads[waited].wait()
            waited += 1
        tops.append(score(n, at))
    for k in range(1, ZONES):
        prepare(k)
    while waited < PARTS:
        loads[waited].wait()
        waited += 1
    spot_copy.wait()

    due = None
    for n, (k, base, size) in enumerate(blocks):
        top = top_of(tops)
        first, final = base == 0, base + size == items
        new = top if first else jnp.maximum(highest, top)
        if drawn is not None:
            new = jnp.maximum(new, drawn - 3e38)
        ahead = subs_of(n + 1)
        tops = []
        count = size // DEPTH
        added = None
        hold = min(count - 1, HOLD) if due is not None else 0
        for q in range(count + 1):
            upto = len(ahead) if q == count else min(len(ahead), LEAD + len(ahead) * max(0, q - hold) // max(1, count - hold))
            if due is not None and q == hold + 1:
                due()
                due = None
            while len(tops) < upto:
                tops.append(score(*ahead[len(tops)]))
            if q < count:
                piece = weigh(n, q * DEPTH, new)
                added = piece if added is None else added + piece
                if n < 2:
                    i = base // DEPTH + q
                    widen(edges[i], edges[i + 1])
                lo, hi = base + q * DEPTH, base + (q + 1) * DEPTH
                lo, hi = [max(0, v - (blocks[1][1] + blocks[1][2])) if k == 0 else v for v in (lo, hi)]
                whole = items - (blocks[1][1] + blocks[1][2] if k == 0 else 0)
                lo, hi = lo * chunk // whole, hi * chunk // whole
                if hi > lo:
                    fetch(k, lo, hi)
                    got = jnp.max(stage[k % 2, lo:hi, :], axis=0, keepdims=True)
                    drawn = jnp.concatenate([got] * (chunk // width), axis=1)
        acc[...] = added if first else acc[...] * jnp.exp2(highest - new) + added
        highest = new
        if final:
            def due(k=k, highest=highest):
                send_out(k, highest, hits(k))
                if k == 2:
                    relay(0)
    due()

    relay(1)
    relay(2)
    last[members + ZONES - 2] = send[ZONES - 1, gx * side + spot]
    for k in range(ZONES):
        most = send.at[k, pl.ds(0, members - 1), used]
        pltpu.make_async_remote_copy(
            src_ref=most, dst_ref=most, send_sem=send_sem, recv_sem=recv_sem.at[k],
            device_id=(gx, gy), device_id_type=MESH).wait_send()
    crossed = last.at[pl.ds(members - 1, ZONES - 1), used]
    cross = pltpu.make_async_remote_copy(
        src_ref=crossed, dst_ref=crossed, send_sem=mid_sem, recv_sem=last_sem,
        device_id=(gx, gy), device_id_type=MESH)
    cross.wait_send()
    arrived(ZONES - 1).wait_recv()
    cross.wait_recv()
    top, total, target, factor = merge(last)
    packed[stat_row:stat_row + 1, :] = top / LOG2E + jnp.log(total) - target
    packed[0:rows, :] = gather(last, factor / total)


def unpack(rows, stat_row, packed, exp_out, nll_out):
    exp_out[...] = packed[0:rows, :]
    nll_out[...] = packed[stat_row, 0:rows]


def solution(mesh):
    n = mesh.size
    ngx, ngy = mesh.shape["gx"], mesh.shape["gy"]

    def local(hidden_states, item_table, targets):
        positions, width = hidden_states.shape
        items = item_table.shape[0]
        rows = positions // n
        side = ngy // ZONES
        members = ngx * side
        chunk = members * rows
        tall = -(-rows // 8) * 8 + 8
        vmem = pl.BlockSpec(memory_space=pltpu.VMEM)
        far = pl.BlockSpec(memory_space=pl.ANY)
        packed = pl.pallas_call(
            functools.partial(kernel, ngx, ngy, rows),
            out_shape=pltpu.VMEM((tall, width), jnp.float32),
            in_specs=[far, far, far],
            out_specs=vmem,
            scratch_shapes=[
                pltpu.VMEM((positions, width), jnp.bfloat16),
                pltpu.VMEM((ZONES, chunk, width), jnp.bfloat16),
                pltpu.VMEM((ZONES, 2 * width, chunk), jnp.bfloat16),
                pltpu.VMEM((positions // width, width), jnp.int32),
                pltpu.VMEM((ZONES * ngx, width), jnp.int32),
                pltpu.SMEM((ZONES * ngx, width), jnp.int32),
                pltpu.VMEM((items, width), jnp.bfloat16),
                pltpu.VMEM((items + 8, width), jnp.float32),
                pltpu.VMEM((width + 16, items), jnp.bfloat16),
                pltpu.VMEM((BLOCK, chunk), jnp.float32),
                pltpu.VMEM((BLOCK, chunk), jnp.float32),
                pltpu.VMEM((2, chunk, width), jnp.float32),
                pltpu.VMEM((width + 16, chunk), jnp.float32),
                pltpu.VMEM((ZONES, members, tall, width), jnp.float32),
                pltpu.VMEM((ZONES - 1, members, tall, width), jnp.float32),
                pltpu.VMEM((ZONES - 1, tall, width), jnp.float32),
                pltpu.VMEM((members + ZONES - 1, tall, width), jnp.float32),
                pltpu.SemaphoreType.DMA,
                pltpu.SemaphoreType.DMA((ZONES,)),
                pltpu.SemaphoreType.DMA,
                pltpu.SemaphoreType.DMA,
                pltpu.SemaphoreType.DMA((PARTS,)),
                pltpu.SemaphoreType.DMA((2,)),
            ],
            compiler_params=pltpu.CompilerParams(collective_id=0, has_side_effects=True, vmem_limit_bytes=60000000),
        )(hidden_states, item_table, targets.reshape(positions // width, width))
        packed = pltpu.with_memory_space_constraint(packed, pltpu.VMEM)
        return pl.pallas_call(
            functools.partial(unpack, rows, tall - 8),
            out_shape=(jax.ShapeDtypeStruct((rows, width), jnp.float32), jax.ShapeDtypeStruct((rows,), jnp.float32)),
            in_specs=[vmem], out_specs=(vmem, vmem),
        )(packed)

    return jax.shard_map(
        local, mesh=mesh,
        in_specs=(P(), P(AXES, None), P()),
        out_specs=(P(AXES, None), P(AXES)),
        check_vma=False,
    )
```

time: 20.7 us -> 19.9 us (0.961)
  Pallas kernels: 19.9 us -> 19.2 us
    pallas_call x1, Pallas kernels: 19.3 us -> 18.5 us  [local(): pl.pallas_call(functools.partial(kernel, ngx, ngy, rows), out_shape=pltpu...]
where the time goes in v2:
time: 19.9 us; the launch traced here: 19.8 us
  Pallas kernels  19.2 us (96%)
  between operations  0.64 us (3%)
    pallas_call x1, Pallas kernels, local(): pl.pallas_call(functools.partial(kernel, ngx, ngy, rows), out_shape=pltpu...  18.5 us
    pallas_call x1, Pallas kernels, local(): pl.pallas_call(functools.partial(unpack, rows, tall - 8), out_shape=(jax....  0.61 us

profile of v2, /device:TPU:0, one launch (start us, length us, event | category | flops | bytes accessed | tf_op | source)
XLA Modules:
  0.0 19.8 jit_solution(1049729132756706078)
XLA Ops:
  0.6 18.5 %shard_map.50.packed = f32[40,128]{1,0:T(8,128)S(1)} custom-call(bf16[1024,128]{1,0:T(8,128)(2,1)} %hid.1, bf16[8192,128]{1,0:T(8,128)(2,1)} %table.1, s32[8,128]{1,0:T(8,128)} %bitcast.1), custom_call_target="tpu_custom_call" | custom-call | tf_op jit(solution)/shard_map/pallas_call | solution.py:303
  19.2 0.6 %shard_map.51 = (f32[32,128]{1,0:T(8,128)}, f32[32]{0:T(128)}) custom-call(f32[40,128]{1,0:T(8,128)S(1)} %shard_map.50.packed), custom_call_target="tpu_custom_call" | custom-call | tf_op jit(solution)/shard_map/pallas_call | solution.py:336

commit v3 on v2

--- a/solution.py
+++ b/solution.py
@@ -57,7 +57,6 @@
     for i in range(PARTS):
         at = pl.ds(i * part, part)
         loads.append(pltpu.make_async_copy(table.at[at], tab.at[at], load_sem.at[i]))
-        loads[i].start()
 
     even[0:8, :] = jnp.zeros((8, chunk), jnp.float32)
     odd[0:8, :] = jnp.zeros((8, chunk), jnp.float32)
@@ -68,6 +67,8 @@
         return c
 
     lax.fori_loop(1, members, greet, 0)
+    for load in loads:
+        load.start()
     for k in range(ZONES - 1):
         pl.semaphore_signal(barrier, inc=1, device_id=twin(k), device_id_type=MESH)
 

time: 19.9 us -> 19.5 us (0.980)
  Pallas kernels: 19.2 us -> 18.7 us
    pallas_call x1, Pallas kernels: 18.5 us -> 18.1 us  [local(): pl.pallas_call(functools.partial(kernel, ngx, ngy, rows), out_shape=pltpu...]
where the time goes in v3:
time: 19.5 us; the launch traced here: 19.3 us
  Pallas kernels  18.7 us (96%)
  between operations  0.64 us (3%)
    pallas_call x1, Pallas kernels, local(): pl.pallas_call(functools.partial(kernel, ngx, ngy, rows), out_shape=pltpu...  18.1 us
    pallas_call x1, Pallas kernels, local(): pl.pallas_call(functools.partial(unpack, rows, tall - 8), out_shape=(jax....  0.61 us

profile of v3, /device:TPU:0, one launch (start us, length us, event | category | flops | bytes accessed | tf_op | source)
XLA Modules:
  0.0 19.3 jit_solution(11660713077463395770)
XLA Ops:
  0.6 18.1 %shard_map.50.packed = f32[40,128]{1,0:T(8,128)S(1)} custom-call(bf16[1024,128]{1,0:T(8,128)(2,1)} %hid.1, bf16[8192,128]{1,0:T(8,128)(2,1)} %table.1, s32[8,128]{1,0:T(8,128)} %bitcast.1), custom_call_target="tpu_custom_call" | custom-call | tf_op jit(solution)/shard_map/pallas_call | solution.py:304
  18.7 0.6 %shard_map.51 = (f32[32,128]{1,0:T(8,128)}, f32[32]{0:T(128)}) custom-call(f32[40,128]{1,0:T(8,128)S(1)} %shard_map.50.packed), custom_call_target="tpu_custom_call" | custom-call | tf_op jit(solution)/shard_map/pallas_call | solution.py:337
